TPU v7x, 32 devices: a whole 2x2x4 slice. The times are simulated.
32 devices in a mesh: pipe: 4 (over z), dp: 4 (over x, core), expert: 2 (over y).
Axes of the slice: x: 2, y: 2, z: 4, core: 2. Of those that a mesh axis runs over, the one named last changes fastest.
Arguments:
- entering: bfloat16 [4, 512, 4096], P('pipe', 'dp', 'expert'), may hold values from -6 to 6
- pending: bfloat16 [4, 512, 4096], P('pipe', 'dp', 'expert'), may hold values from -6 to 6
- stashed_in: bfloat16 [4, 512, 4096], P('pipe', 'dp', 'expert'), may hold values from -6 to 6
- forward_routes: int32 [4, 512, 2], P('pipe', 'dp'), may hold values from 0 to 3, all different within a row; in each aligned block of 128 rows (0 to 127, 128 to 255, ..., all dimensions but the last counted through in order) at most 64 rows name the same one
- backward_routes: int32 [4, 512, 2], P('pipe', 'dp'), may hold values from 0 to 3, all different within a row; in each aligned block of 128 rows (0 to 127, 128 to 255, ..., all dimensions but the last counted through in order) at most 64 rows name the same one
- norm_gains: float32 [4, 4096], P('pipe', 'expert'), may hold values from 0.5 to 1.5
- w_router: bfloat16 [4, 4096, 4], P('pipe', 'expert'), may hold values from -0.09375 to 0.09375
- w_gateup: bfloat16 [4, 4, 4096, 2, 1024], P('pipe', 'dp', None, None, 'expert'), may hold values from -0.09375 to 0.09375
- w_down: bfloat16 [4, 4, 1024, 4096], P('pipe', 'dp', 'expert'), may hold values from -0.1875 to 0.1875
Outputs:
- forward_out: bfloat16 [4, 512, 4096], P('pipe', 'dp', 'expert')
- input_grads: bfloat16 [4, 512, 4096], P('pipe', 'dp', 'expert')
- passed_forward: bfloat16 [4, 512, 4096], P('pipe', 'dp', 'expert')
- passed_backward: bfloat16 [4, 512, 4096], P('pipe', 'dp', 'expert')
- gain_grads: float32 [4, 4096], P('pipe', 'expert')
Inputs may be any that keep to these rules, and one draw needn't show every extreme that they name: `forward_routes`: each row names 2 different experts; in each aligned block of 128 rows (one sequence) every expert is named by exactly 64 rows. `backward_routes`: each row names 2 different experts; in each aligned block of 128 rows (one sequence) every expert is named by exactly 64 rows.
All inputs are finite; a program needn't handle non-finite values.
Results may differ from a plain program's by a relative error of at most 0.015.
Values may be sent and summed in bfloat16 or wider, within the bound.
A program may use at most 64 MiB of HBM per device.

v0:
```python
import jax
import jax.numpy as jnp
from jax import lax
from jax.sharding import PartitionSpec as P

D = 4096
ROUTE_SCALE = 2.827
EPSILON = 1e-05


def shifted(block, axis, distance):
    devices = range(lax.axis_size(axis))
    route = [(i - distance, i) for i in devices if i - distance in devices]
    return lax.ppermute(block, axis, route)


def feature_sum(values):
    return lax.psum(values, "expert")


def normalize(tokens, gain_row):
    values = tokens.astype(jnp.float32)
    squares = feature_sum(jnp.sum(values * values, axis=-1, keepdims=True))
    scaling = lax.rsqrt(squares / D + EPSILON)
    return (values, scaling, (values * scaling * gain_row).astype(jnp.bfloat16))


def gating(moe_in, router, routes):
    experts = router.shape[1]
    logits = feature_sum(jnp.dot(moe_in, router, preferred_element_type=jnp.float32))
    selection = (routes[:, :, None] == jnp.arange(experts, dtype=jnp.int32)[None, None, :]).astype(
        jnp.float32
    )
    chosen = jnp.sum(logits[:, None, :] * selection, axis=-1)
    lifted = jax.nn.sigmoid(chosen)
    lifted_sum = jnp.sum(lifted, axis=-1, keepdims=True)
    return (ROUTE_SCALE * lifted / lifted_sum, lifted, lifted_sum, selection)


def layout(routes, experts):
    capacity = routes.shape[0] * routes.shape[1] // experts
    flattened = routes.reshape(-1)
    member = (flattened[:, None] == jnp.arange(experts, dtype=jnp.int32)[None, :]).astype(jnp.int32)
    before = jnp.cumsum(member, axis=0) - member
    position = jnp.sum(before * member, axis=1)
    destination = flattened * capacity + position
    placing = (
        destination[:, None] == jnp.arange(experts * capacity, dtype=jnp.int32)[None, :]
    ).astype(jnp.bfloat16)
    return (capacity, destination, placing)


def spread(placing, route_rows):
    return jnp.einsum("rc,rd->cd", placing, route_rows, preferred_element_type=jnp.float32).astype(
        jnp.bfloat16
    )


def add_projection(gate_up, segment):
    return jnp.einsum("sxcd,xdkf->sxckf", segment, gate_up, preferred_element_type=jnp.float32)


def run_forward(tokens, routes, gain_row, router, gate_up, down_w):
    length, local_width = tokens.shape
    experts = router.shape[1]
    local_count = gate_up.shape[0]
    values, scaling, moe_in = normalize(tokens, gain_row)
    gate_weights, lifted, lifted_sum, selection = gating(moe_in, router, routes)
    capacity, destination, placing = layout(routes, experts)
    route_rows = jnp.repeat(moe_in, routes.shape[1], axis=0)
    buffer = spread(placing, route_rows).reshape(
        experts // local_count, local_count, capacity, local_width
    )

    def compute(received):
        projected = add_projection(gate_up, lax.all_gather(received, "expert", axis=3, tiled=True))
        gate_pre = projected[:, :, :, 0]
        second = projected[:, :, :, 1]
        inner_act = (jax.nn.silu(gate_pre) * second).astype(jnp.bfloat16)
        partial_value = jnp.einsum(
            "sxcf,xfd->sxcd", inner_act, down_w, preferred_element_type=jnp.float32
        )
        summed = lax.psum_scatter(
            partial_value.astype(jnp.bfloat16), "expert", scatter_dimension=3, tiled=True
        )
        return lax.all_to_all(summed, "dp", split_axis=0, concat_axis=0, tiled=True)

    results = compute(lax.all_to_all(buffer, "dp", split_axis=0, concat_axis=0, tiled=True))
    picked = jnp.take(
        results.reshape(experts * capacity, local_width), destination, axis=0
    ).reshape(length, routes.shape[1], local_width)
    return (values + jnp.sum(gate_weights[:, :, None] * picked.astype(jnp.float32), axis=1)).astype(
        jnp.bfloat16
    )


def run_backward(stashed, incoming, routes, gain_row, router, gate_up, down_w):
    length, local_width = stashed.shape
    experts = router.shape[1]
    local_count = gate_up.shape[0]
    chosen_count = routes.shape[1]
    values, scaling, moe_in = normalize(stashed, gain_row)
    gate_weights, lifted, lifted_sum, selection = gating(moe_in, router, routes)
    capacity, destination, placing = layout(routes, experts)
    slot_shape = (experts // local_count, local_count, capacity, local_width)
    row_buffer = spread(placing, jnp.repeat(moe_in, chosen_count, axis=0)).reshape(slot_shape)
    upstream_buffer = spread(placing, jnp.repeat(incoming, chosen_count, axis=0)).reshape(
        slot_shape
    )

    def compute(received):
        rows_in, up_in = received
        rows_piece = lax.all_gather(rows_in, "expert", axis=3, tiled=True)
        up_piece = lax.all_gather(up_in, "expert", axis=3, tiled=True)
        first_sum = jnp.einsum(
            "sxcd,xdkf->sxckf", rows_piece, gate_up, preferred_element_type=jnp.float32
        )
        second_sum = jnp.einsum(
            "sxcd,xfd->sxcf", up_piece, down_w, preferred_element_type=jnp.float32
        )
        gate_pre = first_sum[:, :, :, 0]
        second = first_sum[:, :, :, 1]
        lifted_act = jax.nn.sigmoid(gate_pre)
        activated = gate_pre * lifted_act
        inner_act = (activated * second).astype(jnp.bfloat16)
        gate_total = feature_sum(
            jnp.sum(inner_act.astype(jnp.float32) * second_sum, axis=-1)
        ).astype(jnp.bfloat16)
        grad_first = (
            second_sum * second * lifted_act * (1.0 + gate_pre * (1.0 - lifted_act))
        ).astype(jnp.bfloat16)
        grad_second = (second_sum * activated).astype(jnp.bfloat16)
        stacked = jnp.stack([grad_first, grad_second], axis=3)
        partial_value = jnp.einsum(
            "sxckf,xdkf->sxcd", stacked, gate_up, preferred_element_type=jnp.float32
        )
        summed = lax.psum_scatter(
            partial_value.astype(jnp.bfloat16), "expert", scatter_dimension=3, tiled=True
        )
        return (
            lax.all_to_all(summed, "dp", split_axis=0, concat_axis=0, tiled=True),
            lax.all_to_all(gate_total, "dp", split_axis=0, concat_axis=0, tiled=True),
        )

    back_rows, back_gate = compute(
        (
            lax.all_to_all(row_buffer, "dp", split_axis=0, concat_axis=0, tiled=True),
            lax.all_to_all(upstream_buffer, "dp", split_axis=0, concat_axis=0, tiled=True),
        )
    )
    back_rows = jnp.take(
        back_rows.reshape(experts * capacity, local_width), destination, axis=0
    ).reshape(length, chosen_count, local_width)
    back_gate = (
        jnp.take(back_gate.reshape(-1), destination, axis=0)
        .reshape(length, chosen_count)
        .astype(jnp.float32)
    )
    moe_cot = jnp.sum(gate_weights[:, :, None] * back_rows.astype(jnp.float32), axis=1).astype(
        jnp.bfloat16
    )
    mixed = jnp.sum(back_gate * lifted, axis=-1, keepdims=True) / lifted_sum
    chosen_cot = ROUTE_SCALE * (back_gate - mixed) / lifted_sum * lifted * (1.0 - lifted)
    logit_cot = jnp.sum(chosen_cot[:, :, None] * selection, axis=1)
    norm_cot = moe_cot.astype(jnp.float32) + jnp.dot(
        logit_cot, router.astype(jnp.float32).T, precision=lax.Precision.HIGHEST
    )
    scaled = norm_cot * gain_row
    inner_product = feature_sum(jnp.sum(scaled * values, axis=-1, keepdims=True))
    token_cot = (
        incoming.astype(jnp.float32)
        + scaling * scaled
        - values * (scaling * scaling * scaling) * inner_product / D
    )
    gain_cot = jnp.sum(norm_cot * values * scaling, axis=0)
    return (token_cot.astype(jnp.bfloat16), gain_cot)


def local(
    entering,
    pending,
    stashed_in,
    forward_routes,
    backward_routes,
    norm_gains,
    w_router,
    w_gateup,
    w_down,
):
    gain_row = norm_gains[0]
    router = w_router[0]
    gate_up = w_gateup[0]
    down_w = w_down[0]
    produced = run_forward(entering[0], forward_routes[0], gain_row, router, gate_up, down_w)
    cotangent, gain_part = run_backward(
        stashed_in[0], pending[0], backward_routes[0], gain_row, router, gate_up, down_w
    )
    passed_forward = shifted(produced, "pipe", 1)
    passed_backward = shifted(cotangent, "pipe", -1)
    gain_total = lax.psum(gain_part, "dp")
    return (
        produced[None],
        cotangent[None],
        passed_forward[None],
        passed_backward[None],
        gain_total[None],
    )


def solution(mesh):
    placed = (
        P("pipe", "dp", "expert"),
        P("pipe", "dp", "expert"),
        P("pipe", "dp", "expert"),
        P("pipe", "dp", None),
        P("pipe", "dp", None),
        P("pipe", "expert"),
        P("pipe", "expert", None),
        P("pipe", "dp", None, None, "expert"),
        P("pipe", "dp", "expert", None),
    )
    return jax.shard_map(
        local,
        mesh=mesh,
        in_specs=placed,
        out_specs=(
            P("pipe", "dp", "expert"),
            P("pipe", "dp", "expert"),
            P("pipe", "dp", "expert"),
            P("pipe", "dp", "expert"),
            P("pipe", "expert"),
        ),
        check_vma=False,
    )
```

profile of v0, /device:TPU:0, one launch (start us, length us, event | category | flops | bytes accessed | tf_op | source)
XLA Modules:
  0.0 331.1 jit_solution(16429123784945353185)
XLA Ops:
  7.2 0.8 copy.106
  8.2 0.1 reshape_squeeze.7
  8.3 1.2 fusion.46
  9.5 5.9 %psum.51 = f32[128,1]{0,1:T(1,128)S(1)} all-reduce(f32[128,1]{0,1:T(1,128)S(1)} %bitcast.284), channel_id=1, replica_groups=mesh['pipe'=4,'dp'=4,'expert'=2] {'expert'}, use_global_device_ids=true, to_apply=%region_11.13 | all-reduce | flops 128 | bytes 1024 | tf_op jit(solution)/shard_map/psum | solution.py:18
  15.4 1.2 fusion.48
  16.7 0.6 broadcast_in_dim.66
  17.3 0.4 reshape.435
  17.8 1.2 reduce-window.16
  19.4 0.6 convolution_convert_fusion.1
  20.0 17.7 %all_to_all.30 = bf16[4,1,64,2048]{3,2,1,0:T(8,128)(2,1)} all-to-all(bf16[4,1,64,2048]{3,2,1,0:T(8,128)(2,1)S(1)} %bitcast.261), channel_id=1, replica_groups=mesh['pipe'=4,'dp'=4,'expert'=2] {'dp'}, dimensions={0} | all-to-all | bytes 2097152 | tf_op jit(solution)/shard_map/all_to_all | solution.py:147
  37.8 0.6 broadcast_in_dim.65
  38.5 0.4 reshape.432
  38.9 0.6 convolution_convert_fusion.2
  39.5 17.6 %all_to_all.31 = bf16[4,1,64,2048]{3,2,1,0:T(8,128)(2,1)} all-to-all(bf16[4,1,64,2048]{3,2,1,0:T(8,128)(2,1)S(1)} %bitcast.262), channel_id=1, replica_groups=mesh['pipe'=4,'dp'=4,'expert'=2] {'dp'}, dimensions={0} | all-to-all | bytes 2097152 | tf_op jit(solution)/shard_map/all_to_all | solution.py:148
  57.1 14.7 %all-gather.8.cloned.1.call-done = bf16[4,1,64,4096]{3,2,0,1:T(8,128)(2,1)} async-done(((bf16[4,1,64,2048]{3,2,0,1:T(8,128)(2,1)}), bf16[4,1,64,4096]{3,2,0,1:T(8,128)(2,1)}) %all-gather.8.cloned.1.call-update) | async-done | bytes 2097168 | tf_op jit(solution)/shard_map/all_gather | solution.py:113
  71.8 6.3 %fusion.26 = f32[4,1,64,2,512]{4,2,0,3,1:T(8,128)S(1)} fusion(bf16[4096,2,512,1]{2,1,0,3:T(2,128)(2,1)} %bitcast.285, bf16[4,1,64,4096]{3,2,0,1:T(8,128)(2,1)} %all-gather.8.cloned.1.call-done), kind=kOutput, calls=%fused_computation.33 | convolution fusion | flops 2147483648 | bytes 11534336 | tf_op jit(solution)/shard_map/sxcd,xdkf->sxckf/dot_general | solution.py:115
  78.1 28.3 %all-gather.6.cloned.1.call-done = bf16[4,1,64,4096]{3,2,0,1:T(8,128)(2,1)} async-done(((bf16[4,1,64,2048]{3,2,0,1:T(8,128)(2,1)}), bf16[4,1,64,4096]{3,2,0,1:T(8,128)(2,1)}) %all-gather.6.cloned.1.call-update) | async-done | bytes 2097168 | tf_op jit(solution)/shard_map/all_gather | solution.py:114
  106.5 4.4 %fusion.82 = (bf16[4,1,64,1,512]{4,2,0,3,1:T(8,128)(2,1)S(1)}, f32[4,64]{1,0:T(4,128)S(1)}, bf16[4,1,64,1,512]{4,2,0,3,1:T(8,128)(2,1)S(1)}) fusion(f32[4,1,64,2,512]{4,2,0,3,1:T(8,128)S(1)} %fusion.26, bf16[1,1,512,4096]{3,2,1,0:T(8,128)(2,1)} %param.19, bf16[4,1,64,4096]{3,2,0,1:T(8,128)(2,1)} %all-gather.6.cloned.1.call-done), kind=kOutput, calls=%fused_computation.89 | convolution fusion | flops 1076100864 | bytes 7865344 | tf_op jit(solution)/shard_map/sxcd,xfd->sxcf/dot_general | solution.py:118
  110.8 7.1 %fusion.14 = bf16[4,1,64,4096]{3,2,0,1:T(8,128)(2,1)} fusion(bf16[4096,2,512,1]{2,1,0,3:T(2,128)(2,1)} %bitcast.286, bf16[4,1,64,1,512]{4,2,0,3,1:T(8,128)(2,1)S(1)} %get-tuple-element.25, bf16[4,1,64,1,512]{4,2,0,3,1:T(8,128)(2,1)S(1)} %get-tuple-element.23), kind=kOutput, calls=%fused_computation.14 | convolution fusion | flops 2148794368 | bytes 11010048 | tf_op jit(solution)/shard_map/sxckf,xdkf->sxcd/dot_general | solution.py:134
  118.1 0.5 copy-done.8
  118.7 0.1 eq.109
  118.9 0.1 reshape_squeeze.6
  119.2 0.1 mul.340
  119.4 1.2 reduce-window.14
  121.1 0.2 fusion.58
  121.3 0.3 fusion.69
  121.6 8.1 %all-reduce.1 = (f32[128,1]{0,1:T(1,128)S(1)}, f32[128,4]{0,1:T(4,128)S(1)}, bf16[4,1,64]{2,1,0:T(2,128)(2,1)}) all-reduce(f32[128,1]{0,1:T(1,128)S(1)} %bitcast.282, f32[128,4]{0,1:T(4,128)S(1)} %fusion.69, f32[4,1,64]{2,1,0:T(1,128)S(1)} %bitcast.283), channel_id=1, replica_groups=mesh['pipe'=4,'dp'=4,'expert'=2] {'expert'}, use_global_device_ids=true, to_apply=%region_1.0 | all-reduce | flops 896 | bytes 6656 | tf_op jit(solution)/shard_map/psum | solution.py:18
  129.7 3.2 all-to-all-start.5
  132.9 3.6 %all-to-all-done.5 = bf16[4,1,64]{2,1,0:T(2,128)(2,1)S(1)} async-done(((bf16[4,1,64]{2,1,0:T(2,128)(2,1)}), bf16[4,1,64]{2,1,0:T(2,128)(2,1)S(1)}, u32[]{:S(2)}, u32[]{:S(2)}) %all-to-all-start.5) | async-done | bytes 544 | tf_op jit(solution)/shard_map/all_to_all | solution.py:142
  136.6 13.9 %reduce-scatter.5.cloned.1.call-done = bf16[4,1,64,2048]{3,2,0,1:T(8,128)(2,1)} async-done(((bf16[4,1,64,4096]{3,2,0,1:T(8,128)(2,1)}), bf16[4,1,64,2048]{3,2,0,1:T(8,128)(2,1)}) %reduce-scatter.5.cloned.1.call-update) | async-done | bytes 1048592 | tf_op jit(solution)/shard_map/reduce_scatter | solution.py:137
  150.5 3.5 %all-to-all-start.4 = ((bf16[4,1,64,2048]{3,2,1,0:T(8,128)(2,1)}), bf16[4,1,64,2048]{3,2,1,0:T(8,128)(2,1)S(1)}, u32[]{:S(2)}, u32[]{:S(2)}) async-start(bf16[4,1,64,2048]{3,2,1,0:T(8,128)(2,1)} %bitcast.265), calls=%async_computation.6 | async-start | bytes 2097152 | tf_op jit(solution)/shard_map/all_to_all | solution.py:141
  154.0 0.2 all-gather.4.cloned.1.call-start
  154.2 0.3 fusion.66
  154.6 1.9 gather_fusion
  156.5 0.2 gather.10
  157.0 11.4 %all-to-all-done.4 = bf16[4,1,64,2048]{3,2,1,0:T(8,128)(2,1)S(1)} async-done(((bf16[4,1,64,2048]{3,2,1,0:T(8,128)(2,1)}), bf16[4,1,64,2048]{3,2,1,0:T(8,128)(2,1)S(1)}, u32[]{:S(2)}, u32[]{:S(2)}) %all-to-all-start.4) | async-done | bytes 1048608 | tf_op jit(solution)/shard_map/all_to_all | solution.py:141
  168.4 2.3 gather_fusion.2
  170.7 1.4 select_convert_fusion
  172.2 2.3 reshape.445
  174.5 4.8 %multiply_reduce_fusion = bf16[128,2048]{1,0:T(8,128)(2,1)S(1)} fusion(f32[128,2,2048]{2,1,0:T(2,128)} %reshape.445, f32[128,2]{1,0:T(8,128)S(1)} %copy.105), kind=kLoop, calls=%fused_computation.25 | loop fusion | flops 786432 | bytes 2622464 | tf_op jit(solution)/shard_map/reduce_sum | solution.py:159
  179.3 1.0 fusion.55
  180.3 4.9 %all-reduce = (f32[128,4]{0,1:T(4,128)S(1)}, f32[128]{0:T(128)S(1)}) all-reduce(f32[128,4]{0,1:T(4,128)S(1)} %fusion.66, f32[128]{0:T(128)S(1)} %get-tuple-element.7), channel_id=1, replica_groups=mesh['pipe'=4,'dp'=4,'expert'=2] {'expert'}, use_global_device_ids=true, to_apply=%region_2.0 | all-reduce | flops 640 | bytes 5120 | tf_op jit(solution)/shard_map/psum | solution.py:18
  185.2 0.5 fusion.52
  185.8 0.6 broadcast_in_dim.36
  186.4 0.4 reshape.425
  186.8 0.6 convolution_convert_fusion.3
  187.4 17.6 %all_to_all.32 = bf16[4,1,64,2048]{3,2,1,0:T(8,128)(2,1)} all-to-all(bf16[4,1,64,2048]{3,2,1,0:T(8,128)(2,1)S(1)} %bitcast.263), channel_id=1, replica_groups=mesh['pipe'=4,'dp'=4,'expert'=2] {'dp'}, dimensions={0} | all-to-all | bytes 2097152 | tf_op jit(solution)/shard_map/all_to_all | solution.py:88
  205.1 32.3 %all-gather.4.cloned.1.call-done = bf16[4,1,64,4096]{3,2,0,1:T(8,128)(2,1)} async-done(((bf16[4,1,64,2048]{3,2,0,1:T(8,128)(2,1)}), bf16[4,1,64,4096]{3,2,0,1:T(8,128)(2,1)}) %all-gather.4.cloned.1.call-update) | async-done | bytes 2097168 | tf_op jit(solution)/shard_map/all_gather | solution.py:76
  237.4 6.5 %fusion.31 = f32[4,1,64,2,512]{4,2,3,0,1:T(8,128)S(1)} fusion(bf16[4096,2,512]{2,1,0:T(2,128)(2,1)} %bitcast.287, bf16[4,1,64,4096]{3,2,0,1:T(8,128)(2,1)} %all-gather.4.cloned.1.call-done), kind=kOutput, calls=%fused_computation.34 | convolution fusion | flops 2147483648 | bytes 11534336 | tf_op jit(solution)/shard_map/sxcd,xdkf->sxckf/dot_general | solution.py:60
  243.9 2.7 fusion.13
  246.6 32.1 %reduce-scatter.3.cloned.1.call-done = bf16[4,1,64,2048]{3,2,0,1:T(8,128)(2,1)} async-done(((bf16[4,1,64,4096]{3,2,0,1:T(8,128)(2,1)}), bf16[4,1,64,2048]{3,2,0,1:T(8,128)(2,1)}) %reduce-scatter.3.cloned.1.call-update) | async-done | bytes 1048592 | tf_op jit(solution)/shard_map/reduce_scatter | solution.py:83
  278.6 3.5 %all-to-all-start.1 = ((bf16[4,1,64,2048]{3,2,1,0:T(8,128)(2,1)}), bf16[4,1,64,2048]{3,2,1,0:T(8,128)(2,1)S(1)}, u32[]{:S(2)}, u32[]{:S(2)}) async-start(bf16[4,1,64,2048]{3,2,1,0:T(8,128)(2,1)} %bitcast.266), calls=%async_computation.2 | async-start | bytes 2097152 | tf_op jit(solution)/shard_map/all_to_all | solution.py:86
  282.4 1.5 collective-permute-start.1
  283.9 12.7 %all-to-all-done.1 = bf16[4,1,64,2048]{3,2,1,0:T(8,128)(2,1)S(1)} async-done(((bf16[4,1,64,2048]{3,2,1,0:T(8,128)(2,1)}), bf16[4,1,64,2048]{3,2,1,0:T(8,128)(2,1)S(1)}, u32[]{:S(2)}, u32[]{:S(2)}) %all-to-all-start.1) | async-done | bytes 1048608 | tf_op jit(solution)/shard_map/all_to_all | solution.py:86
  296.5 2.3 gather_fusion.1
  298.9 1.4 select_convert_fusion.1
  300.3 2.3 reshape.443
  302.6 4.7 %multiply_reduce_fusion.1 = f32[128,2048]{1,0:T(8,128)S(1)} fusion(f32[128,2,2048]{2,1,0:T(2,128)} %reshape.443, f32[128,2]{1,0:T(8,128)S(1)} %copy.96), kind=kLoop, calls=%fused_computation.26 | loop fusion | flops 786432 | bytes 3146752 | tf_op jit(solution)/shard_map/reduce_sum | solution.py:92
  307.5 3.4 %collective-permute-start = (bf16[128,2048]{1,0:T(8,128)(2,1)S(1)}, bf16[128,2048]{1,0:T(8,128)(2,1)S(1)}, u32[]{:S(2)}, u32[]{:S(2)}) collective-permute-start(bf16[128,2048]{1,0:T(8,128)(2,1)S(1)} %fusion.61), channel_id=1, source_target_pairs={{0,8},{8,16},{16,24},{1,9},{9,17},{17,25},{2,10},{10,18},{18,26},{... | collective-permute-start | bytes 1572872 | tf_op jit(solution)/shard_map/ppermute | solution.py:14
  310.9 6.5 %psum.55 = f32[1,2048]{1,0:T(1,128)} all-reduce(f32[1,2048]{1,0:T(1,128)S(1)} %bitcast.277), channel_id=1, replica_groups=mesh['pipe'=4,'dp'=4,'expert'=2] {'dp'}, use_global_device_ids=true, to_apply=%region_27.29 | all-reduce | flops 2048 | bytes 16384 | tf_op jit(solution)/shard_map/psum | solution.py:200
  317.4 0.9 fusion.64
  318.3 3.6 %collective-permute-done = bf16[128,2048]{1,0:T(8,128)(2,1)S(1)} collective-permute-done((bf16[128,2048]{1,0:T(8,128)(2,1)S(1)}, bf16[128,2048]{1,0:T(8,128)(2,1)S(1)}, u32[]{:S(2)}, u32[]{:S(2)}) %collective-permute-start) | collective-permute-done | bytes 524320 | tf_op jit(solution)/shard_map/ppermute | solution.py:14
  321.9 0.8 copy.151
  322.7 1.9 copy.152
  (75 shorter events, 2.4 us)
Async XLA Ops:
  7.2 114.1 %copy-start = (bf16[1,2048,4]{1,2,0:T(4,128)(2,1)S(1)}, bf16[1,2048,4]{1,2,0:T(4,128)(2,1)}, u32[]{:S(2)}) copy-start(bf16[1,2048,4]{1,2,0:T(4,128)(2,1)} %param.17) | copy-start | bytes 49156
  7.2 64.6 %all-gather.8.cloned.1.call-start = ((), (), s32[]{:S(2)}) async-start(), calls=%async_computation.11 | async-start | bytes 3145728 | tf_op jit(solution)/shard_map/all_gather | solution.py:113
  20.0 17.8 %copy-start.3 = (bf16[1,128,2048]{2,1,0:T(8,128)(2,1)S(1)}, bf16[1,128,2048]{2,1,0:T(8,128)(2,1)}, u32[]{:S(2)}) copy-start(bf16[1,128,2048]{2,1,0:T(8,128)(2,1)} %param.12) | copy-start | bytes 1572868
  37.8 68.7 %all-gather.6.cloned.1.call-start = ((), (), s32[]{:S(2)}) async-start(), calls=%async_computation.10 | async-start | bytes 3145728 | tf_op jit(solution)/shard_map/all_gather | solution.py:114
  57.1 93.4 %reduce-scatter.5.cloned.1.call-start = ((), (), s32[]{:S(2)}) async-start(), calls=%async_computation.12 | async-start | bytes 3145728 | tf_op jit(solution)/shard_map/reduce_scatter | solution.py:137
  118.0 0.7 copy-start.8
  118.0 1.1 copy-start.7
  118.0 3.1 copy-start.1
  118.0 3.3 copy-start.2
  118.0 3.3 %copy-start.6 = (f32[1,2048]{1,0:T(1,128)S(1)}, f32[1,2048]{1,0:T(1,128)}, u32[]{:S(2)}) copy-start(f32[1,2048]{1,0:T(1,128)} %param.16) | copy-start | bytes 24580
  129.7 6.9 %all-to-all-start.5 = ((bf16[4,1,64]{2,1,0:T(2,128)(2,1)}), bf16[4,1,64]{2,1,0:T(2,128)(2,1)S(1)}, u32[]{:S(2)}, u32[]{:S(2)}) async-start(bf16[4,1,64]{2,1,0:T(2,128)(2,1)} %get-tuple-element.14), calls=%async_computation.7 | async-start | bytes 4096 | tf_op jit(solution)/shard_map/all_to_all | solution.py:142
  150.5 17.9 %all-to-all-start.4 = ((bf16[4,1,64,2048]{3,2,1,0:T(8,128)(2,1)}), bf16[4,1,64,2048]{3,2,1,0:T(8,128)(2,1)S(1)}, u32[]{:S(2)}, u32[]{:S(2)}) async-start(bf16[4,1,64,2048]{3,2,1,0:T(8,128)(2,1)} %bitcast.265), calls=%async_computation.6 | async-start | bytes 2097152 | tf_op jit(solution)/shard_map/all_to_all | solution.py:141
  154.0 83.4 %all-gather.4.cloned.1.call-start = ((), (), s32[]{:S(2)}) async-start(), calls=%async_computation.8 | async-start | bytes 3145728 | tf_op jit(solution)/shard_map/all_gather | solution.py:76
  174.5 10.8 %copy-start.4 = (bf16[1,128,2048]{2,1,0:T(8,128)(2,1)S(1)}, bf16[1,128,2048]{2,1,0:T(8,128)(2,1)}, u32[]{:S(2)}) copy-start(bf16[1,128,2048]{2,1,0:T(8,128)(2,1)} %param.12) | copy-start | bytes 1572868
  185.7 96.6 %copy-start.5 = (bf16[128,2048]{1,0:T(8,128)(2,1)}, bf16[128,2048]{1,0:T(8,128)(2,1)S(1)}, u32[]{:S(2)}) copy-start(bf16[128,2048]{1,0:T(8,128)(2,1)S(1)} %get-tuple-element.26) | copy-start | bytes 1572868
  205.0 73.6 %reduce-scatter.3.cloned.1.call-start = ((), (), s32[]{:S(2)}) async-start(), calls=%async_computation.9 | async-start | bytes 3145728 | tf_op jit(solution)/shard_map/reduce_scatter | solution.py:83
  237.4 6.5 %copy-start.9 = (bf16[1,1,512,4096]{3,2,1,0:T(8,128)(2,1)S(1)}, bf16[1,1,512,4096]{3,2,1,0:T(8,128)(2,1)}, u32[]{:S(2)}) copy-start(bf16[1,1,512,4096]{3,2,1,0:T(8,128)(2,1)} %param.19) | copy-start | bytes 12582916
  278.6 17.9 %all-to-all-start.1 = ((bf16[4,1,64,2048]{3,2,1,0:T(8,128)(2,1)}), bf16[4,1,64,2048]{3,2,1,0:T(8,128)(2,1)S(1)}, u32[]{:S(2)}, u32[]{:S(2)}) async-start(bf16[4,1,64,2048]{3,2,1,0:T(8,128)(2,1)} %bitcast.266), calls=%async_computation.2 | async-start | bytes 2097152 | tf_op jit(solution)/shard_map/all_to_all | solution.py:86
  282.4 35.0 %collective-permute-start.1 = (bf16[128,2048]{1,0:T(8,128)(2,1)S(1)}, bf16[128,2048]{1,0:T(8,128)(2,1)}, u32[]{:S(2)}, u32[]{:S(2)}) collective-permute-start(bf16[128,2048]{1,0:T(8,128)(2,1)S(1)} %get-tuple-element.26), channel_id=1, source_target_pairs={{8,0},{16,8},{24,16},{9,1},{17,9},{25,17},{10,2},{18,10},{26,18},{... | collective-permute-start | bytes 1572872 | tf_op jit(solution)/shard_map/ppermute | solution.py:14
  307.5 14.4 %collective-permute-start = (bf16[128,2048]{1,0:T(8,128)(2,1)S(1)}, bf16[128,2048]{1,0:T(8,128)(2,1)S(1)}, u32[]{:S(2)}, u32[]{:S(2)}) collective-permute-start(bf16[128,2048]{1,0:T(8,128)(2,1)S(1)} %fusion.61), channel_id=1, source_target_pairs={{0,8},{8,16},{16,24},{1,9},{9,17},{17,25},{2,10},{10,18},{18,26},{... | collective-permute-start | bytes 1572872 | tf_op jit(solution)/shard_map/ppermute | solution.py:14
Sparse Core Ops, SparseCore 0:
  37.9 33.8 all-gather.7
  73.3 33.0 all-gather.5
  118.1 32.2 reduce-scatter.4
  205.1 32.1 all-gather.3
  246.7 31.8 reduce-scatter.2
where the time goes:
time: 332 us; the launch traced here: 331 us
  waiting for transfers between devices  153 us (46%)
  blocking collectives  78.3 us (24%)
  matrix products  30.2 us (9%)
  local copies, waits for them, and re-layouts  20.6 us (6%)
  other arithmetic  19.6 us (6%)
  starting transfers between devices  15.6 us (5%)
  between operations  14.2 us (4%)
    reduce_scatter x2, waiting for transfers between devices, compute(): lax.psum_scatter(partial_value.astype(jnp.bfloat16), 'expert', scatter_di...  45.9 us
    all_gather x1, waiting for transfers between devices, compute(): lax.all_gather(received, 'expert', axis=3, tiled=True)  32.3 us
    all_gather x1, waiting for transfers between devices, compute(): up_piece = lax.all_gather(up_in, 'expert', axis=3, tiled=True)  28.3 us
    psum x3, blocking collectives, feature_sum(): return lax.psum(values, 'expert')  18.9 us
    all_to_all x1, blocking collectives, run_backward(): lax.all_to_all(row_buffer, 'dp', split_axis=0, concat_axis=0, tiled=True)  17.7 us
    all_to_all x1, blocking collectives, run_forward(): lax.all_to_all(buffer, 'dp', split_axis=0, concat_axis=0, tiled=True)  17.6 us
    all_to_all x1, blocking collectives, run_backward(): lax.all_to_all(upstream_buffer, 'dp', split_axis=0, concat_axis=0, tiled=...  17.6 us
    all_gather x1, waiting for transfers between devices, compute(): rows_piece = lax.all_gather(rows_in, 'expert', axis=3, tiled=True)  14.7 us
  transfers between devices with their start and end apart: 10, of which 9 were waited for; matrix products, arithmetic and copies ran while one was open for 8% of the time, Pallas kernels for 0%

commit v1 on v0

--- a/solution.py
+++ b/solution.py
@@ -111,13 +111,25 @@
     def compute(received):
         rows_in, up_in = received
         rows_piece = lax.all_gather(rows_in, "expert", axis=3, tiled=True)
-        up_piece = lax.all_gather(up_in, "expert", axis=3, tiled=True)
         first_sum = jnp.einsum(
             "sxcd,xdkf->sxckf", rows_piece, gate_up, preferred_element_type=jnp.float32
         )
-        second_sum = jnp.einsum(
-            "sxcd,xfd->sxcf", up_piece, down_w, preferred_element_type=jnp.float32
-        )
+        size, index, span = (lax.axis_size("expert"), lax.axis_index("expert"), up_in.shape[3])
+        ahead = [(i_2, (i_2 + 1) % size) for i_2 in range(size)]
+        block_2, total = (up_in, None)
+        for step in range(size):
+            coming = lax.ppermute(block_2, "expert", ahead) if step < size - 1 else None
+            update = jnp.einsum(
+                "sxcd,xfd->sxcf",
+                block_2,
+                lax.dynamic_slice_in_dim(
+                    down_w, (index - step) % size * span, block_2.shape[3], axis=2
+                ),
+                preferred_element_type=jnp.float32,
+            )
+            total = update if total is None else total + update
+            block_2 = coming
+        second_sum = total
         gate_pre = first_sum[:, :, :, 0]
         second = first_sum[:, :, :, 1]
         lifted_act = jax.nn.sigmoid(gate_pre)

time: 332 us -> 316 us (0.952)
  waiting for transfers between devices: 153 us -> 136 us
    all_gather x1 -> x0, waiting for transfers between devices: 28.3 us -> none  [compute(): up_piece = lax.all_gather(up_in, 'expert', axis=3, tiled=True)]
    all_gather x1, waiting for transfers between devices: 14.7 us -> 23.7 us  [compute(): rows_piece = lax.all_gather(rows_in, 'expert', axis=3, tiled=True)]
  transfers between devices with their start and end apart: 10 -> 10, of which waited for: 9 -> 9; matrix products, arithmetic and copies ran while one was open for 8% -> 9% of each run, Pallas kernels for 0% -> 0%
where the time goes in v1:
time: 316 us; the launch traced here: 315 us
  waiting for transfers between devices  136 us (43%)
  blocking collectives  77.6 us (25%)
  matrix products  29.5 us (9%)
  local copies, waits for them, and re-layouts  20.6 us (7%)
  other arithmetic  19.6 us (6%)
  starting transfers between devices  17.6 us (6%)
  between operations  14.2 us (4%)
    reduce_scatter x2, waiting for transfers between devices, compute(): lax.psum_scatter(partial_value.astype(jnp.bfloat16), 'expert', scatter_di...  45.9 us
    all_gather x1, waiting for transfers between devices, compute(): lax.all_gather(received, 'expert', axis=3, tiled=True)  32.3 us
    all_gather x1, waiting for transfers between devices, compute(): rows_piece = lax.all_gather(rows_in, 'expert', axis=3, tiled=True)  23.7 us
    psum x3, blocking collectives, feature_sum(): return lax.psum(values, 'expert')  18.9 us
    all_to_all x1, blocking collectives, run_backward(): lax.all_to_all(row_buffer, 'dp', split_axis=0, concat_axis=0, tiled=True)  17.7 us
    all_to_all x1, blocking collectives, run_forward(): lax.all_to_all(buffer, 'dp', split_axis=0, concat_axis=0, tiled=True)  17.6 us
    all_to_all x1, blocking collectives, run_backward(): lax.all_to_all(upstream_buffer, 'dp', split_axis=0, concat_axis=0, tiled=...  16.9 us
    all_to_all x1, waiting for transfers between devices, compute(): return lax.all_to_all(summed, 'dp', split_axis=0, concat_axis=0, tiled=True)  12.7 us
  transfers between devices with their start and end apart: 10, of which 9 were waited for; matrix products, arithmetic and copies ran while one was open for 9% of the time, Pallas kernels for 0%

profile of v1, /device:TPU:0, one launch (start us, length us, event | category | flops | bytes accessed | tf_op | source)
XLA Modules:
  0.0 315.4 jit_solution(7872391133897873411)
XLA Ops:
  7.2 0.8 copy.106
  8.2 0.1 reshape_squeeze.7
  8.3 1.2 fusion.50
  9.5 5.9 %psum.51 = f32[128,1]{0,1:T(1,128)S(1)} all-reduce(f32[128,1]{0,1:T(1,128)S(1)} %bitcast.293), channel_id=1, replica_groups=mesh['pipe'=4,'dp'=4,'expert'=2] {'expert'}, use_global_device_ids=true, to_apply=%region_11.13 | all-reduce | flops 128 | bytes 1024 | tf_op jit(solution)/shard_map/psum | solution.py:18
  15.4 1.2 fusion.52
  16.7 0.6 broadcast_in_dim.66
  17.3 0.4 reshape.451
  17.8 1.2 reduce-window.16
  19.4 0.6 convolution_convert_fusion.1
  20.0 17.7 %all_to_all.30 = bf16[4,1,64,2048]{3,2,1,0:T(8,128)(2,1)} all-to-all(bf16[4,1,64,2048]{3,2,1,0:T(8,128)(2,1)S(1)} %bitcast.269), channel_id=1, replica_groups=mesh['pipe'=4,'dp'=4,'expert'=2] {'dp'}, dimensions={0} | all-to-all | bytes 2097152 | tf_op jit(solution)/shard_map/all_to_all | solution.py:159
  37.8 0.6 broadcast_in_dim.65
  38.5 0.4 reshape.446
  38.9 0.6 convolution_convert_fusion.2
  39.5 16.9 %all_to_all.31 = bf16[4,1,64,2048]{3,2,1,0:T(8,128)(2,1)S(1)} all-to-all(bf16[4,1,64,2048]{3,2,1,0:T(8,128)(2,1)S(1)} %bitcast.270), channel_id=1, replica_groups=mesh['pipe'=4,'dp'=4,'expert'=2] {'dp'}, dimensions={0} | all-to-all | bytes 2097152 | tf_op jit(solution)/shard_map/all_to_all | solution.py:160
  56.3 2.0 collective-permute-start
  58.3 2.3 fusion.20
  60.7 23.7 %all-gather.5.cloned.1.call-done = bf16[4,1,64,4096]{3,2,0,1:T(8,128)(2,1)} async-done(((bf16[4,1,64,2048]{3,2,0,1:T(8,128)(2,1)}), bf16[4,1,64,4096]{3,2,0,1:T(8,128)(2,1)}) %all-gather.5.cloned.1.call-update) | async-done | bytes 2097168 | tf_op jit(solution)/shard_map/all_gather | solution.py:113
  84.3 6.5 %fusion.29 = f32[4,1,64,2,512]{4,2,0,3,1:T(8,128)S(1)} fusion(bf16[4096,2,512,1]{2,1,0,3:T(2,128)(2,1)} %bitcast.294, bf16[4,1,64,4096]{3,2,0,1:T(8,128)(2,1)} %all-gather.5.cloned.1.call-done), kind=kOutput, calls=%fused_computation.36 | convolution fusion | flops 2147483648 | bytes 11534336 | tf_op jit(solution)/shard_map/sxcd,xdkf->sxckf/dot_general | solution.py:114
  90.8 3.2 %collective-permute-done = bf16[4,1,64,2048]{3,2,0,1:T(8,128)(2,1)S(1)} collective-permute-done((bf16[4,1,64,2048]{3,2,0,1:T(8,128)(2,1)S(1)}, bf16[4,1,64,2048]{3,2,0,1:T(8,128)(2,1)S(1)}, u32[]{:S(2)}, u32[]{:S(2)}) %collective-permute-start) | collective-permute-done | bytes 1048608 | tf_op jit(solution)/shard_map/ppermute | solution.py:121
  94.1 1.2 fusion.88
  95.2 7.1 %fusion.14 = bf16[4,1,64,4096]{3,2,0,1:T(8,128)(2,1)} fusion(bf16[4096,2,512,1]{2,1,0,3:T(2,128)(2,1)} %bitcast.295, bf16[4,1,64,1,512]{4,2,0,3,1:T(8,128)(2,1)S(1)} %get-tuple-element.25, bf16[4,1,64,1,512]{4,2,0,3,1:T(8,128)(2,1)S(1)} %get-tuple-element.23), kind=kOutput, calls=%fused_computation.14 | convolution fusion | flops 2148794368 | bytes 11010048 | tf_op jit(solution)/shard_map/sxckf,xdkf->sxcd/dot_general | solution.py:146
  102.5 0.5 copy-done.8
  103.3 0.1 reshape_squeeze.6
  103.7 1.2 reduce-window.14
  105.4 0.2 fusion.62
  105.7 0.3 fusion.75
  106.0 8.1 %all-reduce.1 = (f32[128,1]{0,1:T(1,128)S(1)}, f32[128,4]{0,1:T(4,128)S(1)}, bf16[4,1,64]{2,1,0:T(2,128)(2,1)}) all-reduce(f32[128,1]{0,1:T(1,128)S(1)} %bitcast.291, f32[128,4]{0,1:T(4,128)S(1)} %fusion.75, f32[4,1,64]{2,1,0:T(1,128)S(1)} %bitcast.292), channel_id=1, replica_groups=mesh['pipe'=4,'dp'=4,'expert'=2] {'expert'}, use_global_device_ids=true, to_apply=%region_1.0 | all-reduce | flops 896 | bytes 6656 | tf_op jit(solution)/shard_map/psum | solution.py:18
  114.1 3.2 %all-to-all-start.5 = ((bf16[4,1,64]{2,1,0:T(2,128)(2,1)}), bf16[4,1,64]{2,1,0:T(2,128)(2,1)S(1)}, u32[]{:S(2)}, u32[]{:S(2)}) async-start(bf16[4,1,64]{2,1,0:T(2,128)(2,1)} %get-tuple-element.14), calls=%async_computation.7 | async-start | bytes 4096 | tf_op jit(solution)/shard_map/all_to_all | solution.py:154
  117.3 3.6 %all-to-all-done.5 = bf16[4,1,64]{2,1,0:T(2,128)(2,1)S(1)} async-done(((bf16[4,1,64]{2,1,0:T(2,128)(2,1)}), bf16[4,1,64]{2,1,0:T(2,128)(2,1)S(1)}, u32[]{:S(2)}, u32[]{:S(2)}) %all-to-all-start.5) | async-done | bytes 544 | tf_op jit(solution)/shard_map/all_to_all | solution.py:154
  121.0 13.9 %reduce-scatter.5.cloned.1.call-done = bf16[4,1,64,2048]{3,2,0,1:T(8,128)(2,1)} async-done(((bf16[4,1,64,4096]{3,2,0,1:T(8,128)(2,1)}), bf16[4,1,64,2048]{3,2,0,1:T(8,128)(2,1)}) %reduce-scatter.5.cloned.1.call-update) | async-done | bytes 1048592 | tf_op jit(solution)/shard_map/reduce_scatter | solution.py:149
  134.8 3.5 %all-to-all-start.4 = ((bf16[4,1,64,2048]{3,2,1,0:T(8,128)(2,1)}), bf16[4,1,64,2048]{3,2,1,0:T(8,128)(2,1)S(1)}, u32[]{:S(2)}, u32[]{:S(2)}) async-start(bf16[4,1,64,2048]{3,2,1,0:T(8,128)(2,1)} %bitcast.273), calls=%async_computation.6 | async-start | bytes 2097152 | tf_op jit(solution)/shard_map/all_to_all | solution.py:153
  138.4 0.2 all-gather.3.cloned.1.call-start
  138.6 0.3 fusion.72
  139.0 1.9 gather_fusion
  140.9 0.2 gather.10
  141.3 11.4 %all-to-all-done.4 = bf16[4,1,64,2048]{3,2,1,0:T(8,128)(2,1)S(1)} async-done(((bf16[4,1,64,2048]{3,2,1,0:T(8,128)(2,1)}), bf16[4,1,64,2048]{3,2,1,0:T(8,128)(2,1)S(1)}, u32[]{:S(2)}, u32[]{:S(2)}) %all-to-all-start.4) | async-done | bytes 1048608 | tf_op jit(solution)/shard_map/all_to_all | solution.py:153
  152.8 2.3 gather_fusion.2
  155.1 1.4 select_convert_fusion
  156.5 2.3 reshape.461
  158.9 4.8 %multiply_reduce_fusion = bf16[128,2048]{1,0:T(8,128)(2,1)S(1)} fusion(f32[128,2,2048]{2,1,0:T(2,128)} %reshape.461, f32[128,2]{1,0:T(8,128)S(1)} %copy.105), kind=kLoop, calls=%fused_computation.26 | loop fusion | flops 786432 | bytes 2622464 | tf_op jit(solution)/shard_map/reduce_sum | solution.py:171
  163.7 1.0 fusion.59
  164.7 4.9 %all-reduce = (f32[128,4]{0,1:T(4,128)S(1)}, f32[128]{0:T(128)S(1)}) all-reduce(f32[128,4]{0,1:T(4,128)S(1)} %fusion.72, f32[128]{0:T(128)S(1)} %get-tuple-element.7), channel_id=1, replica_groups=mesh['pipe'=4,'dp'=4,'expert'=2] {'expert'}, use_global_device_ids=true, to_apply=%region_2.0 | all-reduce | flops 640 | bytes 5120 | tf_op jit(solution)/shard_map/psum | solution.py:18
  169.6 0.5 fusion.56
  170.1 0.6 broadcast_in_dim.36
  170.8 0.4 reshape.438
  171.2 0.6 convolution_convert_fusion.3
  171.8 17.6 %all_to_all.32 = bf16[4,1,64,2048]{3,2,1,0:T(8,128)(2,1)} all-to-all(bf16[4,1,64,2048]{3,2,1,0:T(8,128)(2,1)S(1)} %bitcast.271), channel_id=1, replica_groups=mesh['pipe'=4,'dp'=4,'expert'=2] {'dp'}, dimensions={0} | all-to-all | bytes 2097152 | tf_op jit(solution)/shard_map/all_to_all | solution.py:88
  189.5 32.3 %all-gather.3.cloned.1.call-done = bf16[4,1,64,4096]{3,2,0,1:T(8,128)(2,1)} async-done(((bf16[4,1,64,2048]{3,2,0,1:T(8,128)(2,1)}), bf16[4,1,64,4096]{3,2,0,1:T(8,128)(2,1)}) %all-gather.3.cloned.1.call-update) | async-done | bytes 2097168 | tf_op jit(solution)/shard_map/all_gather | solution.py:76
  221.8 6.5 %fusion.34 = f32[4,1,64,2,512]{4,2,3,0,1:T(8,128)S(1)} fusion(bf16[4096,2,512]{2,1,0:T(2,128)(2,1)} %bitcast.296, bf16[4,1,64,4096]{3,2,0,1:T(8,128)(2,1)} %all-gather.3.cloned.1.call-done), kind=kOutput, calls=%fused_computation.37 | convolution fusion | flops 2147483648 | bytes 11534336 | tf_op jit(solution)/shard_map/sxcd,xdkf->sxckf/dot_general | solution.py:60
  228.3 2.7 fusion.13
  230.9 32.1 %reduce-scatter.3.cloned.1.call-done = bf16[4,1,64,2048]{3,2,0,1:T(8,128)(2,1)} async-done(((bf16[4,1,64,4096]{3,2,0,1:T(8,128)(2,1)}), bf16[4,1,64,2048]{3,2,0,1:T(8,128)(2,1)}) %reduce-scatter.3.cloned.1.call-update) | async-done | bytes 1048592 | tf_op jit(solution)/shard_map/reduce_scatter | solution.py:83
  263.0 3.5 %all-to-all-start.1 = ((bf16[4,1,64,2048]{3,2,1,0:T(8,128)(2,1)}), bf16[4,1,64,2048]{3,2,1,0:T(8,128)(2,1)S(1)}, u32[]{:S(2)}, u32[]{:S(2)}) async-start(bf16[4,1,64,2048]{3,2,1,0:T(8,128)(2,1)} %bitcast.275), calls=%async_computation.2 | async-start | bytes 2097152 | tf_op jit(solution)/shard_map/all_to_all | solution.py:86
  266.7 1.5 collective-permute-start.2
  268.3 12.7 %all-to-all-done.1 = bf16[4,1,64,2048]{3,2,1,0:T(8,128)(2,1)S(1)} async-done(((bf16[4,1,64,2048]{3,2,1,0:T(8,128)(2,1)}), bf16[4,1,64,2048]{3,2,1,0:T(8,128)(2,1)S(1)}, u32[]{:S(2)}, u32[]{:S(2)}) %all-to-all-start.1) | async-done | bytes 1048608 | tf_op jit(solution)/shard_map/all_to_all | solution.py:86
  280.9 2.3 gather_fusion.1
  283.3 1.4 select_convert_fusion.1
  284.7 2.3 reshape.459
  287.0 4.7 %multiply_reduce_fusion.1 = f32[128,2048]{1,0:T(8,128)S(1)} fusion(f32[128,2,2048]{2,1,0:T(2,128)} %reshape.459, f32[128,2]{1,0:T(8,128)S(1)} %copy.96), kind=kLoop, calls=%fused_computation.29 | loop fusion | flops 786432 | bytes 3146752 | tf_op jit(solution)/shard_map/reduce_sum | solution.py:92
  291.9 3.4 %collective-permute-start.1 = (bf16[128,2048]{1,0:T(8,128)(2,1)S(1)}, bf16[128,2048]{1,0:T(8,128)(2,1)S(1)}, u32[]{:S(2)}, u32[]{:S(2)}) collective-permute-start(bf16[128,2048]{1,0:T(8,128)(2,1)S(1)} %fusion.65), channel_id=1, source_target_pairs={{0,8},{8,16},{16,24},{1,9},{9,17},{17,25},{2,10},{10,18},{18,26},{... | collective-permute-start | bytes 1572872 | tf_op jit(solution)/shard_map/ppermute | solution.py:14
  295.3 6.5 %psum.55 = f32[1,2048]{1,0:T(1,128)} all-reduce(f32[1,2048]{1,0:T(1,128)S(1)} %bitcast.286), channel_id=1, replica_groups=mesh['pipe'=4,'dp'=4,'expert'=2] {'dp'}, use_global_device_ids=true, to_apply=%region_27.29 | all-reduce | flops 2048 | bytes 16384 | tf_op jit(solution)/shard_map/psum | solution.py:212
  301.8 0.9 fusion.68
  302.7 3.6 %collective-permute-done.1 = bf16[128,2048]{1,0:T(8,128)(2,1)S(1)} collective-permute-done((bf16[128,2048]{1,0:T(8,128)(2,1)S(1)}, bf16[128,2048]{1,0:T(8,128)(2,1)S(1)}, u32[]{:S(2)}, u32[]{:S(2)}) %collective-permute-start.1) | collective-permute-done | bytes 524320 | tf_op jit(solution)/shard_map/ppermute | solution.py:14
  306.2 0.8 copy.151
  307.0 1.9 copy.152
  (77 shorter events, 2.7 us)
Async XLA Ops:
  7.2 98.5 %copy-start = (bf16[1,2048,4]{1,2,0:T(4,128)(2,1)S(1)}, bf16[1,2048,4]{1,2,0:T(4,128)(2,1)}, u32[]{:S(2)}) copy-start(bf16[1,2048,4]{1,2,0:T(4,128)(2,1)} %param.17) | copy-start | bytes 49156
  7.2 77.2 %all-gather.5.cloned.1.call-start = ((), (), s32[]{:S(2)}) async-start(), calls=%async_computation.10 | async-start | bytes 3145728 | tf_op jit(solution)/shard_map/all_gather | solution.py:113
  20.0 17.8 %copy-start.3 = (bf16[1,128,2048]{2,1,0:T(8,128)(2,1)S(1)}, bf16[1,128,2048]{2,1,0:T(8,128)(2,1)}, u32[]{:S(2)}) copy-start(bf16[1,128,2048]{2,1,0:T(8,128)(2,1)} %param.12) | copy-start | bytes 1572868
  37.8 97.1 %reduce-scatter.5.cloned.1.call-start = ((), (), s32[]{:S(2)}) async-start(), calls=%async_computation.11 | async-start | bytes 3145728 | tf_op jit(solution)/shard_map/reduce_scatter | solution.py:149
  56.3 37.7 %collective-permute-start = (bf16[4,1,64,2048]{3,2,0,1:T(8,128)(2,1)S(1)}, bf16[4,1,64,2048]{3,2,0,1:T(8,128)(2,1)S(1)}, u32[]{:S(2)}, u32[]{:S(2)}) collective-permute-start(bf16[4,1,64,2048]{3,2,0,1:T(8,128)(2,1)S(1)} %bitcast.274), channel_id=1, source_target_pairs={{0,1},{1,0},{2,3},{3,2},{4,5},{5,4},{6,7},{7,6},{8,9},{9,8},{10,11... | collective-permute-start | bytes 3145736 | tf_op jit(solution)/shard_map/ppermute | solution.py:121
  84.3 9.7 %copy-start.9 = (bf16[1,1,512,4096]{3,2,1,0:T(8,128)(2,1)S(1)}, bf16[1,1,512,4096]{3,2,1,0:T(8,128)(2,1)}, u32[]{:S(2)}) copy-start(bf16[1,1,512,4096]{3,2,1,0:T(8,128)(2,1)} %param.19) | copy-start | bytes 12582916
  102.3 0.7 copy-start.8
  102.3 1.1 copy-start.7
  102.3 3.1 copy-start.1
  102.3 3.3 %copy-start.2 = (bf16[1,128,2048]{2,1,0:T(8,128)(2,1)S(1)}, bf16[1,128,2048]{2,1,0:T(8,128)(2,1)}, u32[]{:S(2)}) copy-start(bf16[1,128,2048]{2,1,0:T(8,128)(2,1)} %param.13) | copy-start | bytes 1572868
  102.3 3.3 %copy-start.6 = (f32[1,2048]{1,0:T(1,128)S(1)}, f32[1,2048]{1,0:T(1,128)}, u32[]{:S(2)}) copy-start(f32[1,2048]{1,0:T(1,128)} %param.16) | copy-start | bytes 24580
  114.1 6.9 %all-to-all-start.5 = ((bf16[4,1,64]{2,1,0:T(2,128)(2,1)}), bf16[4,1,64]{2,1,0:T(2,128)(2,1)S(1)}, u32[]{:S(2)}, u32[]{:S(2)}) async-start(bf16[4,1,64]{2,1,0:T(2,128)(2,1)} %get-tuple-element.14), calls=%async_computation.7 | async-start | bytes 4096 | tf_op jit(solution)/shard_map/all_to_all | solution.py:154
  134.8 17.9 %all-to-all-start.4 = ((bf16[4,1,64,2048]{3,2,1,0:T(8,128)(2,1)}), bf16[4,1,64,2048]{3,2,1,0:T(8,128)(2,1)S(1)}, u32[]{:S(2)}, u32[]{:S(2)}) async-start(bf16[4,1,64,2048]{3,2,1,0:T(8,128)(2,1)} %bitcast.273), calls=%async_computation.6 | async-start | bytes 2097152 | tf_op jit(solution)/shard_map/all_to_all | solution.py:153
  138.4 83.4 %all-gather.3.cloned.1.call-start = ((), (), s32[]{:S(2)}) async-start(), calls=%async_computation.8 | async-start | bytes 3145728 | tf_op jit(solution)/shard_map/all_gather | solution.py:76
  158.8 10.8 %copy-start.4 = (bf16[1,128,2048]{2,1,0:T(8,128)(2,1)S(1)}, bf16[1,128,2048]{2,1,0:T(8,128)(2,1)}, u32[]{:S(2)}) copy-start(bf16[1,128,2048]{2,1,0:T(8,128)(2,1)} %param.12) | copy-start | bytes 1572868
  170.1 96.6 %copy-start.5 = (bf16[128,2048]{1,0:T(8,128)(2,1)}, bf16[128,2048]{1,0:T(8,128)(2,1)S(1)}, u32[]{:S(2)}) copy-start(bf16[128,2048]{1,0:T(8,128)(2,1)S(1)} %get-tuple-element.26) | copy-start | bytes 1572868
  189.4 73.6 %reduce-scatter.3.cloned.1.call-start = ((), (), s32[]{:S(2)}) async-start(), calls=%async_computation.9 | async-start | bytes 3145728 | tf_op jit(solution)/shard_map/reduce_scatter | solution.py:83
  221.8 6.5 %copy-start.10 = (bf16[1,1,512,4096]{3,2,1,0:T(8,128)(2,1)S(1)}, bf16[1,1,512,4096]{3,2,1,0:T(8,128)(2,1)}, u32[]{:S(2)}) copy-start(bf16[1,1,512,4096]{3,2,1,0:T(8,128)(2,1)} %param.19) | copy-start | bytes 12582916
  263.0 17.9 %all-to-all-start.1 = ((bf16[4,1,64,2048]{3,2,1,0:T(8,128)(2,1)}), bf16[4,1,64,2048]{3,2,1,0:T(8,128)(2,1)S(1)}, u32[]{:S(2)}, u32[]{:S(2)}) async-start(bf16[4,1,64,2048]{3,2,1,0:T(8,128)(2,1)} %bitcast.275), calls=%async_computation.2 | async-start | bytes 2097152 | tf_op jit(solution)/shard_map/all_to_all | solution.py:86
  266.7 35.0 %collective-permute-start.2 = (bf16[128,2048]{1,0:T(8,128)(2,1)S(1)}, bf16[128,2048]{1,0:T(8,128)(2,1)}, u32[]{:S(2)}, u32[]{:S(2)}) collective-permute-start(bf16[128,2048]{1,0:T(8,128)(2,1)S(1)} %get-tuple-element.26), channel_id=1, source_target_pairs={{8,0},{16,8},{24,16},{9,1},{17,9},{25,17},{10,2},{18,10},{26,18},{... | collective-permute-start | bytes 1572872 | tf_op jit(solution)/shard_map/ppermute | solution.py:14
  291.9 14.4 %collective-permute-start.1 = (bf16[128,2048]{1,0:T(8,128)(2,1)S(1)}, bf16[128,2048]{1,0:T(8,128)(2,1)S(1)}, u32[]{:S(2)}, u32[]{:S(2)}) collective-permute-start(bf16[128,2048]{1,0:T(8,128)(2,1)S(1)} %fusion.65), channel_id=1, source_target_pairs={{0,8},{8,16},{16,24},{1,9},{9,17},{17,25},{2,10},{10,18},{18,26},{... | collective-permute-start | bytes 1572872 | tf_op jit(solution)/shard_map/ppermute | solution.py:14
Sparse Core Ops, SparseCore 0:
  37.9 46.4 all-gather.4
  102.5 32.2 reduce-scatter.4
  189.5 32.1 all-gather.2
  231.1 31.8 reduce-scatter.2
